TPU v7x, 32 devices: a whole 2x2x4 slice. The times are simulated.
32 devices in a mesh: section: 4 (over y, core), tensor: 8 (over z, x).
Axes of the slice: x: 2, y: 2, z: 4, core: 2. Of those that a mesh axis runs over, the one named last changes fastest.
Arguments:
- saved_inputs: bfloat16 [4, 4, 256, 1024], P('section', None, 'tensor'), may hold values from -6 to 6
- slot_index: int32 [4, 3], P('section'), may hold values from 0 to 3
- example_lengths: int32 [4, 3, 2], P('section'), may hold values from 1 to 192, 256 in all within a row
- first_grads: bfloat16 [4, 256, 1024], P('section', 'tensor'), may hold values from -6 to 6
- loss_grads: bfloat16 [2, 256, 1024], P(None, 'tensor'), may hold values from -6 to 6
- w_in: bfloat16 [4, 1024, 32768], P('section', None, 'tensor'), may hold values from -0.1875 to 0.1875
- w_out: bfloat16 [4, 32768, 1024], P('section', 'tensor'), may hold values from -0.03125 to 0.03125
Outputs:
- grad_in: bfloat16 [4, 1024, 32768], P('section', None, 'tensor')
- grad_out: bfloat16 [4, 32768, 1024], P('section', 'tensor')
- input_grads: bfloat16 [4, 3, 256, 1024], P('section', None, 'tensor')
Inputs may be any that keep to these rules, and one draw needn't show every extreme that they name: `example_lengths`: the 2 lengths of one microbatch sum to 256.
All inputs are finite; a program needn't handle non-finite values.
Results may differ from a plain program's by a relative error of at most 0.0095.
Values may be sent and summed in bfloat16 or wider, within the bound.
A program may use at most 128 MiB of HBM per device.

v0:
```python
import jax
import jax.numpy as jnp
from jax import lax
from jax.sharding import PartitionSpec as P

D = 1024
FF = 32768
GAMMA = 0.01


def shifted(value, axis, steps):
    count = lax.axis_size(axis)
    first, last = (max(0, -steps), min(count, count - steps))
    return lax.ppermute(value, axis, [(source, source + steps) for source in range(first, last)])


def membership(lengths, tokens):
    ends = jnp.cumsum(lengths)
    position = jnp.arange(tokens, dtype=jnp.int32)
    example_id = jnp.sum((position[:, None] >= ends[None, :-1]).astype(jnp.int32), axis=1)
    labels = jnp.arange(lengths.shape[0], dtype=jnp.int32)
    return (example_id[:, None] == labels[None, :]).astype(jnp.float32)


def per_device(saved_inputs, slot_index, example_lengths, first_grads, loss_grads, w_in, w_out):
    section_count = lax.axis_size("section")
    is_last = lax.axis_index("section") == section_count - 1
    first = w_in[0]
    second = w_out[0]
    slot_count = loss_grads.shape[0] + 1
    rows = first_grads.shape[1]
    picked = [
        lax.dynamic_index_in_dim(saved_inputs[0], slot_index[0, slot], 0, keepdims=False)
        for slot in range(slot_count)
    ]
    every_input = lax.all_gather(jnp.stack(picked), "tensor", axis=1, tiled=True)
    acc_first = jnp.zeros(first.shape, jnp.float32)
    acc_second = jnp.zeros(second.shape, jnp.float32)
    incoming = first_grads[0]
    results = []
    for slot in range(slot_count):
        inputs = every_input[slot]
        grads = lax.all_gather(incoming, "tensor", axis=0, tiled=True)
        z = jnp.dot(inputs, first, preferred_element_type=jnp.float32)
        relu = jnp.maximum(z, 0.0)
        hidden = (relu * relu).astype(jnp.bfloat16)
        back = jnp.einsum("td,fd->tf", grads, second, preferred_element_type=jnp.float32)
        dz = (2.0 * relu * back).astype(jnp.bfloat16)
        own_terms = jnp.einsum("tf,df->td", dz, first, preferred_element_type=jnp.float32)
        summed = lax.psum(own_terms, "tensor")
        shares = lax.dynamic_slice_in_dim(summed, lax.axis_index("tensor") * rows, rows, 0)
        member = membership(example_lengths[0, slot], inputs.shape[0])
        pieces = []
        for example in range(member.shape[1]):
            keep = member[:, example][:, None].astype(jnp.bfloat16)
            per_first = jnp.einsum(
                "td,tf->df", inputs * keep, dz, preferred_element_type=jnp.float32
            )
            per_second = jnp.einsum(
                "tf,td->fd", hidden, grads * keep, preferred_element_type=jnp.float32
            )
            pieces.append(jnp.sum(per_first * per_first) + jnp.sum(per_second * per_second))
        local_squares = jnp.stack(pieces)
        squares = lax.psum(local_squares, "tensor")
        factor = 1.0 / (jnp.sqrt(squares / (D * FF)) + GAMMA)
        token_factor = jnp.sum(member * factor[None, :], axis=1)
        dzc = (dz.astype(jnp.float32) * token_factor[:, None]).astype(jnp.bfloat16)
        dyc = (grads.astype(jnp.float32) * token_factor[:, None]).astype(jnp.bfloat16)
        acc_first = acc_first + jnp.einsum(
            "td,tf->df", inputs, dzc, preferred_element_type=jnp.float32
        )
        acc_second = acc_second + jnp.einsum(
            "tf,td->fd", hidden, dyc, preferred_element_type=jnp.float32
        )
        passing = (incoming.astype(jnp.float32) + shares).astype(jnp.bfloat16)
        results.append(passing)
        if slot + 1 < slot_count:
            arrived = shifted(passing, "section", -1)
            incoming = jnp.where(is_last, loss_grads[slot], arrived)
    grad_in = acc_first.astype(jnp.bfloat16)[None]
    grad_out = acc_second.astype(jnp.bfloat16)[None]
    input_grads = jnp.stack(results)[None]
    return (grad_in, grad_out, input_grads)


def solution(mesh):
    return jax.shard_map(
        per_device,
        mesh=mesh,
        in_specs=(
            P("section", None, "tensor", None),
            P("section", None),
            P("section", None, None),
            P("section", "tensor", None),
            P(None, "tensor", None),
            P("section", None, "tensor"),
            P("section", "tensor", None),
        ),
        out_specs=(
            P("section", None, "tensor"),
            P("section", "tensor", None),
            P("section", None, "tensor", None),
        ),
        check_vma=False,
    )
```

profile of v0, /device:TPU:0, one launch (start us, length us, event | category | flops | bytes accessed | tf_op | source)
XLA Modules:
  0.0 492.9 jit_solution(11279649531270042013)
XLA Ops:
  7.2 0.0 all-gather.3.cloned.1.call-start
  7.2 1.4 fusion.83
  14.4 0.9 dynamic-slice_bitcast_fusion.2
  15.3 0.7 pad_maximum_fusion
  16.0 0.0 all-gather.3.cloned.1.call-update
  16.0 0.0 all-reduce.5.cloned.1.call-start
  16.1 1.0 slice_reduce_fusion.6
  17.1 0.2 reduce-window.14
  17.3 0.2 reduce-window.10
  17.5 0.2 reduce-window.11
  17.9 34.0 %all-gather = bf16[1,256,1024]{2,1,0:T(8,128)(2,1)S(1)} all-gather(bf16[1,32,1024]{2,1,0:T(8,128)(2,1)} %param.10), channel_id=2, replica_groups=mesh['section'=4,'tensor'=8] {'tensor'}, dimensions={1}, use_global_device_ids=true | all-gather | bytes 589824 | tf_op jit(solution)/shard_map/all_gather | solution.py:43
  51.9 12.3 %all-gather.3.cloned.1.call-done = bf16[3,256,1024]{2,1,0:T(8,128)(2,1)} async-done(((bf16[3,32,1024]{2,1,0:T(8,128)(2,1)}), bf16[3,256,1024]{2,1,0:T(8,128)(2,1)}) %all-gather.3.cloned.1.call-update) | async-done | bytes 1572880 | tf_op jit(solution)/shard_map/all_gather | solution.py:36
  64.2 5.9 %fusion.20 = f32[256,4096]{1,0:T(8,128)S(1)} fusion(bf16[1,1024,4096]{2,1,0:T(8,128)(2,1)} %param.12, bf16[3,256,1024]{2,1,0:T(8,128)(2,1)} %all-gather.3.cloned.1.call-done), kind=kOutput, calls=%fused_computation.34 | convolution fusion | flops 2148532224 | bytes 13107200 | tf_op jit(solution)/shard_map/dot_general | solution.py:44
  70.2 5.2 %multiply_reduce_fusion.8 = f32[]{:T(128)} fusion(bf16[1,256,1024]{2,1,0:T(8,128)(2,1)S(1)} %all-gather, bf16[256]{0:T(256)(128)(2,1)S(1)} %get-tuple-element.11, f32[256,4096]{1,0:T(8,128)S(1)} %fusion.20), kind=kOutput, calls=%fused_computation.10 | convolution fusion | flops 2158231552 | bytes 4719108 | tf_op jit(solution)/shard_map/tf,td->fd/dot_general | solution.py:59
  75.4 5.2 %multiply_reduce_fusion.10 = f32[]{:T(128)} fusion(bf16[1,256,1024]{2,1,0:T(8,128)(2,1)S(1)} %all-gather, bf16[256]{0:T(256)(128)(2,1)S(1)} %get-tuple-element.10, f32[256,4096]{1,0:T(8,128)S(1)} %fusion.20), kind=kOutput, calls=%fused_computation.12 | convolution fusion | flops 2158231552 | bytes 4719108 | tf_op jit(solution)/shard_map/tf,td->fd/dot_general | solution.py:59
  80.6 13.6 %fusion.44 = bf16[256,4096]{1,0:T(8,128)(2,1)S(1)} fusion(bf16[1,4096,1024]{2,1,0:T(8,128)(2,1)S(1)} %bitcast.137, f32[256,4096]{1,0:T(8,128)S(1)} %fusion.20, bf16[1,256,1024]{2,1,0:T(8,128)(2,1)S(1)} %all-gather), kind=kOutput, calls=%fused_computation.42 | convolution fusion | flops 2150629376 | bytes 15204352 | tf_op jit(solution)/shard_map/td,fd->tf/dot_general | solution.py:47
  94.2 7.5 %fusion.12 = f32[256,1024]{1,0:T(8,128)} fusion(bf16[256,4096]{1,0:T(8,128)(2,1)S(1)} %fusion.44, bf16[1,1024,4096]{2,1,0:T(8,128)(2,1)} %param.12), kind=kOutput, calls=%fused_computation.26 | convolution fusion | flops 2147483648 | bytes 11534336 | tf_op jit(solution)/shard_map/tf,df->td/dot_general | solution.py:49
  101.7 0.0 all-reduce.5.cloned.1.call-update
  101.7 0.0 all-reduce.7.cloned.1.call-start
  101.8 6.3 %multiply_reduce_fusion.9 = f32[]{:T(128)} fusion(bf16[256,4096]{1,0:T(8,128)(2,1)S(1)} %fusion.44, bf16[3,256,1024]{2,1,0:T(8,128)(2,1)} %all-gather.3.cloned.1.call-done, bf16[256]{0:T(256)(128)(2,1)S(1)} %get-tuple-element.11), kind=kOutput, calls=%fused_computation.11 | convolution fusion | flops 2156134400 | bytes 2621956 | tf_op jit(solution)/shard_map/td,tf->df/dot_general | solution.py:56
  109.4 6.3 %multiply_reduce_fusion.11 = f32[]{:T(128)} fusion(bf16[256,4096]{1,0:T(8,128)(2,1)S(1)} %fusion.44, bf16[3,256,1024]{2,1,0:T(8,128)(2,1)} %all-gather.3.cloned.1.call-done, bf16[256]{0:T(256)(128)(2,1)S(1)} %get-tuple-element.10), kind=kOutput, calls=%fused_computation.13 | convolution fusion | flops 2156134400 | bytes 2621956 | tf_op jit(solution)/shard_map/td,tf->df/dot_general | solution.py:56
  117.0 8.0 %fusion.26 = f32[256,4096]{1,0:T(8,128)} fusion(bf16[1,1024,4096]{2,1,0:T(8,128)(2,1)} %param.12, bf16[3,256,1024]{2,1,0:T(8,128)(2,1)} %all-gather.3.cloned.1.call-done), kind=kOutput, calls=%fused_computation.36 | convolution fusion | flops 2148532224 | bytes 13107200 | tf_op jit(solution)/shard_map/dot_general | solution.py:44
  125.0 8.5 %fusion.23 = f32[256,4096]{1,0:T(8,128)} fusion(bf16[1,1024,4096]{2,1,0:T(8,128)(2,1)} %param.12, bf16[3,256,1024]{2,1,0:T(8,128)(2,1)} %all-gather.3.cloned.1.call-done), kind=kOutput, calls=%fused_computation.35 | convolution fusion | flops 2148532224 | bytes 13107200 | tf_op jit(solution)/shard_map/dot_general | solution.py:44
  133.5 45.7 %all-reduce.5.cloned.1.call-done = f32[256,1024]{1,0:T(8,128)} async-done(((f32[256,1024]{1,0:T(8,128)}), f32[256,1024]{1,0:T(8,128)}) %all-reduce.5.cloned.1.call-update) | async-done | bytes 1048592 | tf_op jit(solution)/shard_map/psum | solution.py:50
  179.2 0.9 fusion.81
  180.1 1.3 collective-permute-start
  181.4 0.1 pad_maximum_fusion.1
  181.5 1.8 collective-permute-done
  183.2 31.3 %all_gather.14 = bf16[256,1024]{1,0:T(8,128)(2,1)S(1)} all-gather(bf16[32,1024]{1,0:T(8,128)(2,1)S(1)} %bitcast_select_fusion.1), channel_id=1, replica_groups=mesh['section'=4,'tensor'=8] {'tensor'}, dimensions={0}, use_global_device_ids=true | all-gather | bytes 589824 | tf_op jit(solution)/shard_map/all_gather | solution.py:43
  214.5 7.2 %fusion.41 = bf16[256,4096]{1,0:T(8,128)(2,1)S(1)} fusion(bf16[256,1024]{1,0:T(8,128)(2,1)S(1)} %all_gather.14, bf16[1,4096,1024]{2,1,0:T(8,128)(2,1)} %param.13, f32[256,4096]{1,0:T(8,128)} %fusion.23), kind=kOutput, calls=%fused_computation.41 | convolution fusion | flops 2150629376 | bytes 15204352 | tf_op jit(solution)/shard_map/td,fd->tf/dot_general | solution.py:47
  221.8 5.2 %multiply_reduce_fusion.4 = f32[]{:T(128)} fusion(bf16[256,1024]{1,0:T(8,128)(2,1)S(1)} %all_gather.14, bf16[256]{0:T(256)(128)(2,1)S(1)} %get-tuple-element.9, f32[256,4096]{1,0:T(8,128)S(1)} %copy-done.2), kind=kOutput, calls=%fused_computation.6 | convolution fusion | flops 2158231552 | bytes 4719108 | tf_op jit(solution)/shard_map/tf,td->fd/dot_general | solution.py:59
  226.9 6.8 %fusion.8 = f32[256,1024]{1,0:T(8,128)} fusion(bf16[256,4096]{1,0:T(8,128)(2,1)S(1)} %fusion.41, bf16[1,1024,4096]{2,1,0:T(8,128)(2,1)} %param.12), kind=kOutput, calls=%fused_computation.22 | convolution fusion | flops 2147483648 | bytes 11534336 | tf_op jit(solution)/shard_map/tf,df->td/dot_general | solution.py:49
  233.7 0.0 all-reduce.7.cloned.1.call-update
  233.7 0.2 all-reduce.9.cloned.1.call-start
  234.0 6.3 %multiply_reduce_fusion.5 = f32[]{:T(128)} fusion(bf16[256,4096]{1,0:T(8,128)(2,1)S(1)} %fusion.41, bf16[3,256,1024]{2,1,0:T(8,128)(2,1)} %all-gather.3.cloned.1.call-done, bf16[256]{0:T(256)(128)(2,1)S(1)} %get-tuple-element.9), kind=kOutput, calls=%fused_computation.7 | convolution fusion | flops 2156134400 | bytes 2621956 | tf_op jit(solution)/shard_map/td,tf->df/dot_general | solution.py:56
  241.5 6.5 %multiply_reduce_fusion.7 = f32[]{:T(128)} fusion(bf16[256,4096]{1,0:T(8,128)(2,1)S(1)} %fusion.41, bf16[3,256,1024]{2,1,0:T(8,128)(2,1)} %all-gather.3.cloned.1.call-done, bf16[256]{0:T(256)(128)(2,1)S(1)} %get-tuple-element.8), kind=kOutput, calls=%fused_computation.9 | convolution fusion | flops 2156134400 | bytes 2621956 | tf_op jit(solution)/shard_map/td,tf->df/dot_general | solution.py:56
  248.0 5.6 %multiply_reduce_fusion.6 = f32[]{:T(128)} fusion(bf16[256,1024]{1,0:T(8,128)(2,1)S(1)} %all_gather.14, bf16[256]{0:T(256)(128)(2,1)S(1)} %get-tuple-element.8, f32[256,4096]{1,0:T(8,128)S(1)} %copy-done.3), kind=kOutput, calls=%fused_computation.8 | convolution fusion | flops 2158231552 | bytes 4719108 | tf_op jit(solution)/shard_map/tf,td->fd/dot_general | solution.py:59
  254.9 57.6 %all-reduce.7.cloned.1.call-done = f32[256,1024]{1,0:T(8,128)} async-done(((f32[256,1024]{1,0:T(8,128)}), f32[256,1024]{1,0:T(8,128)}) %all-reduce.7.cloned.1.call-update) | async-done | bytes 1048592 | tf_op jit(solution)/shard_map/psum | solution.py:50
  312.5 0.9 add_convert_fusion.3
  313.4 1.3 collective-permute-start.1
  314.7 0.1 pad_maximum_fusion.2
  314.8 1.8 collective-permute-done.1
  316.6 31.3 %all_gather.15 = bf16[256,1024]{1,0:T(8,128)(2,1)S(1)} all-gather(bf16[32,1024]{1,0:T(8,128)(2,1)S(1)} %bitcast_select_fusion), channel_id=1, replica_groups=mesh['section'=4,'tensor'=8] {'tensor'}, dimensions={0}, use_global_device_ids=true | all-gather | bytes 589824 | tf_op jit(solution)/shard_map/all_gather | solution.py:43
  347.9 7.1 %fusion.38 = bf16[256,4096]{1,0:T(8,128)(2,1)S(1)} fusion(bf16[256,1024]{1,0:T(8,128)(2,1)S(1)} %all_gather.15, bf16[1,4096,1024]{2,1,0:T(8,128)(2,1)} %param.13, f32[256,4096]{1,0:T(8,128)} %fusion.26), kind=kOutput, calls=%fused_computation.40 | convolution fusion | flops 2150629376 | bytes 15204352 | tf_op jit(solution)/shard_map/td,fd->tf/dot_general | solution.py:47
  355.0 5.2 %multiply_reduce_fusion = f32[]{:T(128)} fusion(bf16[256,1024]{1,0:T(8,128)(2,1)S(1)} %all_gather.15, bf16[256]{0:T(256)(128)(2,1)S(1)} %get-tuple-element.4, f32[256,4096]{1,0:T(8,128)S(1)} %copy-done.4), kind=kOutput, calls=%fused_computation.2 | convolution fusion | flops 2158231552 | bytes 4719108 | tf_op jit(solution)/shard_map/tf,td->fd/dot_general | solution.py:59
  360.2 5.2 %multiply_reduce_fusion.2 = f32[]{:T(128)} fusion(bf16[256,1024]{1,0:T(8,128)(2,1)S(1)} %all_gather.15, bf16[256]{0:T(256)(128)(2,1)S(1)} %get-tuple-element.3, f32[256,4096]{1,0:T(8,128)S(1)} %copy-done.4), kind=kOutput, calls=%fused_computation.4 | convolution fusion | flops 2158231552 | bytes 4719108 | tf_op jit(solution)/shard_map/tf,td->fd/dot_general | solution.py:59
  365.4 6.5 %multiply_reduce_fusion.1 = f32[]{:T(128)} fusion(bf16[256,4096]{1,0:T(8,128)(2,1)S(1)} %fusion.38, bf16[3,256,1024]{2,1,0:T(8,128)(2,1)} %all-gather.3.cloned.1.call-done, bf16[256]{0:T(256)(128)(2,1)S(1)} %get-tuple-element.4), kind=kOutput, calls=%fused_computation.3 | convolution fusion | flops 2156134400 | bytes 2621956 | tf_op jit(solution)/shard_map/td,tf->df/dot_general | solution.py:56
  373.1 6.3 %multiply_reduce_fusion.3 = f32[]{:T(128)} fusion(bf16[256,4096]{1,0:T(8,128)(2,1)S(1)} %fusion.38, bf16[3,256,1024]{2,1,0:T(8,128)(2,1)} %all-gather.3.cloned.1.call-done, bf16[256]{0:T(256)(128)(2,1)S(1)} %get-tuple-element.3), kind=kOutput, calls=%fused_computation.5 | convolution fusion | flops 2156134400 | bytes 2621956 | tf_op jit(solution)/shard_map/td,tf->df/dot_general | solution.py:56
  380.7 0.1 pad_maximum_fusion.3
  380.7 6.7 %fusion.6 = f32[256,1024]{1,0:T(8,128)} fusion(bf16[256,4096]{1,0:T(8,128)(2,1)S(1)} %fusion.38, bf16[1,1024,4096]{2,1,0:T(8,128)(2,1)} %param.12), kind=kOutput, calls=%fused_computation.20 | convolution fusion | flops 2147483648 | bytes 11534336 | tf_op jit(solution)/shard_map/tf,df->td/dot_general | solution.py:49
  387.5 20.4 %all-reduce = (f32[2]{0:T(128)S(1)}, f32[2]{0:T(128)S(1)}, f32[2]{0:T(128)S(1)}) all-reduce(f32[2]{0:T(128)S(1)} %pad_maximum_fusion.1, f32[2]{0:T(128)S(1)} %pad_maximum_fusion.2, f32[2]{0:T(128)S(1)} %pad_maximum_fusion.3), channel_id=1, replica_groups=mesh['section'=4,'tensor'=8] {'tensor'}, use_global_device_ids=true, to_apply=%region_5.6 | all-reduce | flops 6 | bytes 48 | tf_op jit(solution)/shard_map/psum | solution.py:64
  407.9 0.1 select_reduce_fusion.2
  408.0 0.1 select_reduce_fusion
  408.1 0.1 select_reduce_fusion.1
  408.2 0.0 all-reduce.9.cloned.1.call-update
  408.2 10.6 %fusion.53 = f32[4096,1024]{1,0:T(8,128)} fusion(bf16[256,1024]{1,0:T(8,128)(2,1)} %copy-done.5, f32[256]{0:T(256)S(1)} %select_reduce_fusion.1, f32[256,4096]{1,0:T(8,128)} %fusion.23), kind=kOutput, calls=%fused_computation.58 | convolution fusion | flops 2150367232 | bytes 21496832 | tf_op jit(solution)/shard_map/tf,td->fd/dot_general | solution.py:72
  418.8 8.2 %fusion.52 = f32[4096,1024]{1,0:T(8,128)} fusion(bf16[1,256,1024]{2,1,0:T(8,128)(2,1)S(1)} %all-gather, f32[256]{0:T(256)S(1)} %select_reduce_fusion.2, f32[256,4096]{1,0:T(8,128)S(1)} %copy-done.1), kind=kOutput, calls=%fused_computation.57 | convolution fusion | flops 2150367232 | bytes 21496832 | tf_op jit(solution)/shard_map/tf,td->fd/dot_general | solution.py:72
  427.0 16.7 %fusion.19 = bf16[1,4096,1024]{2,1,0:T(8,128)(2,1)} fusion(f32[4096,1024]{1,0:T(8,128)} %fusion.52, f32[4096,1024]{1,0:T(8,128)} %fusion.53, bf16[256,1024]{1,0:T(8,128)(2,1)S(1)} %all_gather.15, f32[256]{0:T(256)S(1)} %select_reduce_fusion, f32[256,4096]{1,0:T(8,128)} %fusion.26), kind=kOutput, calls=%fused_computation.33 | convolution fusion | flops 2162950144 | bytes 46662656 | tf_op jit(solution)/shard_map/tf,td->fd/dot_general | solution.py:72
  443.8 10.1 %fusion.47 = f32[1024,4096]{1,0:T(8,128)} fusion(bf16[256,4096]{1,0:T(8,128)(2,1)} %copy-done.6, f32[256]{0:T(256)S(1)} %select_reduce_fusion.2, bf16[3,256,1024]{2,1,0:T(8,128)(2,1)} %all-gather.3.cloned.1.call-done), kind=kOutput, calls=%fused_computation.49 | convolution fusion | flops 2150629376 | bytes 19399680 | tf_op jit(solution)/shard_map/td,tf->df/dot_general | solution.py:69
  453.9 9.3 %fusion.48 = f32[1024,4096]{1,0:T(8,128)} fusion(bf16[256,4096]{1,0:T(8,128)(2,1)S(1)} %copy-done.8, f32[256]{0:T(256)S(1)} %select_reduce_fusion.1, bf16[3,256,1024]{2,1,0:T(8,128)(2,1)} %all-gather.3.cloned.1.call-done), kind=kOutput, calls=%fused_computation.50 | convolution fusion | flops 2150629376 | bytes 19399680 | tf_op jit(solution)/shard_map/td,tf->df/dot_general | solution.py:69
  463.1 16.0 %fusion.18 = bf16[1,1024,4096]{2,1,0:T(8,128)(2,1)} fusion(f32[1024,4096]{1,0:T(8,128)} %fusion.47, f32[1024,4096]{1,0:T(8,128)} %fusion.48, bf16[256,4096]{1,0:T(8,128)(2,1)S(1)} %fusion.38, f32[256]{0:T(256)S(1)} %select_reduce_fusion, bf16[3,256,1024]{2,1,0:T(8,128)(2,1)} %all-gather.3.cloned.1.call-done), kind=kOutput, calls=%fused_computation.32 | convolution fusion | flops 2163212288 | bytes 44565504 | tf_op jit(solution)/shard_map/td,tf->df/dot_general | solution.py:69
  479.2 5.2 %all-reduce.9.cloned.1.call-done = f32[256,1024]{1,0:T(8,128)} async-done(((f32[256,1024]{1,0:T(8,128)}), f32[256,1024]{1,0:T(8,128)}) %all-reduce.9.cloned.1.call-update) | async-done | bytes 1048592 | tf_op jit(solution)/shard_map/psum | solution.py:50
  484.3 0.9 fusion.82
  485.2 0.7 maximum_bitcast_fusion
  (40 shorter events, 0.3 us)
Async XLA Ops:
  7.2 57.0 %all-gather.3.cloned.1.call-start = ((), (), s32[]{:S(2)}) async-start(), calls=%async_computation | async-start | bytes 1769472 | tf_op jit(solution)/shard_map/all_gather | solution.py:36
  16.0 163.1 %all-reduce.5.cloned.1.call-start = ((), (), s32[]{:S(2)}) async-start(), calls=%async_computation.1 | async-start | bytes 2097152 | tf_op jit(solution)/shard_map/psum | solution.py:50
  70.1 10.4 %copy-start = (f32[256,4096]{1,0:T(8,128)}, f32[256,4096]{1,0:T(8,128)S(1)}, u32[]{:S(2)}) copy-start(f32[256,4096]{1,0:T(8,128)S(1)} %fusion.20) | copy-start | bytes 12582916
  70.2 10.4 %slice-start = ((s8[8388608]{0:T(1024)(128)(4,1)}), s8[4194304]{0:T(1024)(128)(4,1)S(1)}, s32[]{:S(2)}) async-start(s8[8388608]{0:T(1024)(128)(4,1)} %bitcast.136), calls=%async_computation.4 | async-start | bytes 8388608
  75.4 5.2 %slice-start.1 = ((s8[8388608]{0:T(1024)(128)(4,1)}), s8[4194304]{0:T(1024)(128)(4,1)S(1)}, s32[]{:S(2)}) async-start(s8[8388608]{0:T(1024)(128)(4,1)} %bitcast.136), calls=%async_computation.5 | async-start | bytes 8388608
  94.2 15.2 %copy-start.6 = (bf16[256,4096]{1,0:T(8,128)(2,1)}, bf16[256,4096]{1,0:T(8,128)(2,1)S(1)}, u32[]{:S(2)}) copy-start(bf16[256,4096]{1,0:T(8,128)(2,1)S(1)} %fusion.44) | copy-start | bytes 6291460
  101.7 210.8 %all-reduce.7.cloned.1.call-start = ((), (), s32[]{:S(2)}) async-start(), calls=%async_computation.2 | async-start | bytes 2097152 | tf_op jit(solution)/shard_map/psum | solution.py:50
  125.0 54.2 %copy-start.9 = (bf16[1,32,1024]{2,1,0:T(8,128)(2,1)S(1)}, bf16[1,32,1024]{2,1,0:T(8,128)(2,1)}, u32[]{:S(2)}) copy-start(bf16[1,32,1024]{2,1,0:T(8,128)(2,1)} %param.10) | copy-start | bytes 196612
  125.0 58.3 %copy-start.10 = (bf16[2,32,1024]{2,1,0:T(8,128)(2,1)S(1)}, bf16[2,32,1024]{2,1,0:T(8,128)(2,1)}, u32[]{:S(2)}) copy-start(bf16[2,32,1024]{2,1,0:T(8,128)(2,1)} %param.11) | copy-start | bytes 393220
  180.1 3.1 collective-permute-start
  214.5 33.5 %copy-start.5 = (bf16[256,1024]{1,0:T(8,128)(2,1)}, bf16[256,1024]{1,0:T(8,128)(2,1)S(1)}, u32[]{:S(2)}) copy-start(bf16[256,1024]{1,0:T(8,128)(2,1)S(1)} %all_gather.14) | copy-start | bytes 1572868
  214.5 7.2 %copy-start.2 = (f32[256,4096]{1,0:T(8,128)S(1)}, f32[256,4096]{1,0:T(8,128)}, u32[]{:S(2)}) copy-start(f32[256,4096]{1,0:T(8,128)} %fusion.23) | copy-start | bytes 12582916
  221.7 19.7 %copy-start.7 = (bf16[256,4096]{1,0:T(8,128)(2,1)}, bf16[256,4096]{1,0:T(8,128)(2,1)S(1)}, u32[]{:S(2)}) copy-start(bf16[256,4096]{1,0:T(8,128)(2,1)S(1)} %fusion.41) | copy-start | bytes 6291460
  233.7 250.6 %all-reduce.9.cloned.1.call-start = ((), (), s32[]{:S(2)}) async-start(), calls=%async_computation.3 | async-start | bytes 2097152 | tf_op jit(solution)/shard_map/psum | solution.py:50
  241.5 6.5 %copy-start.3 = (f32[256,4096]{1,0:T(8,128)S(1)}, f32[256,4096]{1,0:T(8,128)}, u32[]{:S(2)}) copy-start(f32[256,4096]{1,0:T(8,128)} %fusion.23) | copy-start | bytes 12582916
  313.4 3.1 collective-permute-start.1
  347.9 7.1 %copy-start.4 = (f32[256,4096]{1,0:T(8,128)S(1)}, f32[256,4096]{1,0:T(8,128)}, u32[]{:S(2)}) copy-start(f32[256,4096]{1,0:T(8,128)} %fusion.26) | copy-start | bytes 12582916
  408.2 10.6 %copy-start.1 = (f32[256,4096]{1,0:T(8,128)S(1)}, f32[256,4096]{1,0:T(8,128)}, u32[]{:S(2)}) copy-start(f32[256,4096]{1,0:T(8,128)} %copy-done) | copy-start | bytes 12582916
  443.8 10.1 %copy-start.8 = (bf16[256,4096]{1,0:T(8,128)(2,1)S(1)}, bf16[256,4096]{1,0:T(8,128)(2,1)}, u32[]{:S(2)}) copy-start(bf16[256,4096]{1,0:T(8,128)(2,1)} %copy-done.7) | copy-start | bytes 6291460
Sparse Core Ops, SparseCore 0:
  16.2 48.0 all-gather.2
  101.8 77.2 all-reduce.4
  233.8 78.5 all-reduce.6
  408.3 75.9 all-reduce.8
where the time goes:
time: 503 us; the launch traced here: 493 us
  matrix products  212 us (42%)
  waiting for transfers between devices  124 us (25%)
  blocking collectives  117 us (23%)
  between operations  27.8 us (6%)
  other arithmetic  5.36 us (1%)
    psum x3, waiting for transfers between devices, per_device(): summed = lax.psum(own_terms, 'tensor')  108 us
    all_gather x3, blocking collectives, per_device(): grads = lax.all_gather(incoming, 'tensor', axis=0, tiled=True)  96.6 us
    dot_general x6, matrix products, per_device(): jnp.einsum('td,tf->df', inputs * keep, dz, preferred_element_type=jnp.flo...  38.2 us
    dot_general x3, matrix products, per_device(): jnp.einsum('tf,td->fd', hidden, dyc, preferred_element_type=jnp.float32)  35.6 us
    dot_general x3, matrix products, per_device(): jnp.einsum('td,tf->df', inputs, dzc, preferred_element_type=jnp.float32)  35.4 us
    dot_general x6, matrix products, per_device(): jnp.einsum('tf,td->fd', hidden, grads * keep, preferred_element_type=jnp....  31.6 us
    dot_general x3, matrix products, per_device(): jnp.einsum('td,fd->tf', grads, second, preferred_element_type=jnp.float32)  27.9 us
    dot_general x3, matrix products, per_device(): z = jnp.dot(inputs, first, preferred_element_type=jnp.float32)  22.4 us
  transfers between devices with their start and end apart: 6, of which 6 were waited for; matrix products, arithmetic and copies ran while one was open for 24% of the time, Pallas kernels for 0%

commit v1 on v0

--- a/solution.py
+++ b/solution.py
@@ -47,7 +47,7 @@
         back = jnp.einsum("td,fd->tf", grads, second, preferred_element_type=jnp.float32)
         dz = (2.0 * relu * back).astype(jnp.bfloat16)
         own_terms = jnp.einsum("tf,df->td", dz, first, preferred_element_type=jnp.float32)
-        summed = lax.psum(own_terms, "tensor")
+        summed = jnp.sum(lax.all_gather(own_terms, "tensor"), axis=0)
         shares = lax.dynamic_slice_in_dim(summed, lax.axis_index("tensor") * rows, rows, 0)
         member = membership(example_lengths[0, slot], inputs.shape[0])
         pieces = []

time: 503 us -> 626 us (1.24)
  waiting for transfers between devices: 124 us -> 259 us
  matrix products: 212 us -> 191 us
  other arithmetic: 5.36 us -> 15.9 us
    all_gather x0 -> x3, waiting for transfers between devices: none -> 246 us  [per_device(): summed = jnp.sum(lax.all_gather(own_terms, 'tensor'), axis=0)]
    psum x3 -> x0, waiting for transfers between devices: 108 us -> none  [per_device(): summed = lax.psum(own_terms, 'tensor')]
    dot_general x3, matrix products: 27.9 us -> 12.2 us  [per_device(): jnp.einsum('td,fd->tf', grads, second, preferred_element_type=jnp.float32)]
    reduce_sum x0 -> x3, other arithmetic: none -> 13.2 us  [per_device(): summed = jnp.sum(lax.all_gather(own_terms, 'tensor'), axis=0)]
  transfers between devices with their start and end apart: 6 -> 6, of which waited for: 6 -> 3; matrix products, arithmetic and copies ran while one was open for 24% -> 25% of each run, Pallas kernels for 0% -> 0%
where the time goes in v1:
time: 626 us; the launch traced here: 619 us
  waiting for transfers between devices  259 us (41%)
  matrix products  191 us (31%)
  blocking collectives  117 us (19%)
  between operations  27.7 us (4%)
  other arithmetic  15.9 us (3%)
    all_gather x3, waiting for transfers between devices, per_device(): summed = jnp.sum(lax.all_gather(own_terms, 'tensor'), axis=0)  246 us
    all_gather x3, blocking collectives, per_device(): grads = lax.all_gather(incoming, 'tensor', axis=0, tiled=True)  97.4 us
    dot_general x6, matrix products, per_device(): jnp.einsum('td,tf->df', inputs * keep, dz, preferred_element_type=jnp.flo...  41.9 us
    dot_general x3, matrix products, per_device(): jnp.einsum('td,tf->df', inputs, dzc, preferred_element_type=jnp.float32)  35.1 us
    dot_general x3, matrix products, per_device(): jnp.einsum('tf,td->fd', hidden, dyc, preferred_element_type=jnp.float32)  33.2 us
    dot_general x6, matrix products, per_device(): jnp.einsum('tf,td->fd', hidden, grads * keep, preferred_element_type=jnp....  32.3 us
    psum x1, blocking collectives, per_device(): squares = lax.psum(local_squares, 'tensor')  19.2 us
    dot_general x3, matrix products, per_device(): z = jnp.dot(inputs, first, preferred_element_type=jnp.float32)  19 us
  transfers between devices with their start and end apart: 6, of which 3 were waited for; matrix products, arithmetic and copies ran while one was open for 25% of the time, Pallas kernels for 0%

profile of v1, /device:TPU:0, one launch (start us, length us, event | category | flops | bytes accessed | tf_op | source)
XLA Modules:
  0.0 618.8 jit_solution(7736907273237496806)
XLA Ops:
  7.2 0.0 all-gather.9.cloned.1.call-start
  7.2 1.4 fusion.83
  14.4 0.9 dynamic-slice_bitcast_fusion.2
  15.3 0.7 pad_maximum_fusion
  16.0 0.0 all-gather.9.cloned.1.call-update
  16.0 0.0 all-gather.11.cloned.1.call-start
  16.1 34.0 %all-gather = bf16[1,256,1024]{2,1,0:T(8,128)(2,1)S(1)} all-gather(bf16[1,32,1024]{2,1,0:T(8,128)(2,1)} %param.10), channel_id=2, replica_groups=mesh['section'=4,'tensor'=8] {'tensor'}, dimensions={1}, use_global_device_ids=true | all-gather | bytes 589824 | tf_op jit(solution)/shard_map/all_gather | solution.py:43
  50.0 13.8 %all-gather.9.cloned.1.call-done = bf16[3,256,1024]{2,1,0:T(8,128)(2,1)} async-done(((bf16[3,32,1024]{2,1,0:T(8,128)(2,1)}), bf16[3,256,1024]{2,1,0:T(8,128)(2,1)}) %all-gather.9.cloned.1.call-update) | async-done | bytes 1572880 | tf_op jit(solution)/shard_map/all_gather | solution.py:36
  63.9 6.0 fusion.20
  70.0 0.0 slice-start.5
  70.0 7.4 %fusion.44 = bf16[256,4096]{1,0:T(8,128)(2,1)S(1)} fusion(bf16[1,4096,1024]{2,1,0:T(8,128)(2,1)} %param.13, f32[256,4096]{1,0:T(8,128)S(1)} %fusion.20, bf16[1,256,1024]{2,1,0:T(8,128)(2,1)S(1)} %all-gather), kind=kOutput, calls=%fused_computation.42 | convolution fusion | flops 2150629376 | bytes 15204352 | tf_op jit(solution)/shard_map/td,fd->tf/dot_general | solution.py:47
  77.4 1.3 copy-done.15
  78.7 3.3 fusion.12
  82.1 0.0 all-gather.11.cloned.1.call-update
  82.1 0.0 all-gather.13.cloned.1.call-start
  82.1 123.6 %all-gather.11.cloned.1.call-done = f32[2048,1024]{1,0:T(8,128)} async-done(((f32[256,1024]{1,0:T(8,128)}), f32[2048,1024]{1,0:T(8,128)}) %all-gather.11.cloned.1.call-update) | async-done | bytes 8388624 | tf_op jit(solution)/shard_map/all_gather | solution.py:50
  205.8 4.5 reduce_sum.179
  210.4 1.6 collective-permute-start
  211.9 6.5 %fusion.23 = f32[256,4096]{1,0:T(8,128)S(1)} fusion(bf16[1,1024,4096]{2,1,0:T(8,128)(2,1)} %param.12, bf16[3,256,1024]{2,1,0:T(8,128)(2,1)S(1)} %copy-done.18), kind=kOutput, calls=%fused_computation.35 | convolution fusion | flops 2148532224 | bytes 13107200 | tf_op jit(solution)/shard_map/dot_general | solution.py:44
  218.5 31.7 %all_gather.34 = bf16[256,1024]{1,0:T(8,128)(2,1)S(1)} all-gather(bf16[32,1024]{1,0:T(8,128)(2,1)S(1)} %bitcast_select_fusion.1), channel_id=1, replica_groups=mesh['section'=4,'tensor'=8] {'tensor'}, dimensions={0}, use_global_device_ids=true | all-gather | bytes 589824 | tf_op jit(solution)/shard_map/all_gather | solution.py:43
  250.2 2.4 fusion.41
  252.6 1.3 copy-done.16
  253.9 6.8 %fusion.8 = f32[256,1024]{1,0:T(8,128)} fusion(bf16[256,4096]{1,0:T(8,128)(2,1)S(1)} %fusion.41, bf16[1,1024,4096]{2,1,0:T(8,128)(2,1)} %param.12), kind=kOutput, calls=%fused_computation.22 | convolution fusion | flops 2147483648 | bytes 11534336 | tf_op jit(solution)/shard_map/tf,df->td/dot_general | solution.py:49
  260.7 0.0 all-gather.13.cloned.1.call-update
  260.7 0.0 all-gather.15.cloned.1.call-start
  260.8 0.2 slice_reduce_fusion.6
  261.0 0.2 reduce-window.14
  261.2 0.2 reduce-window.10
  261.4 0.2 reduce-window.11
  261.7 121.9 %all-gather.13.cloned.1.call-done = f32[2048,1024]{1,0:T(8,128)} async-done(((f32[256,1024]{1,0:T(8,128)}), f32[2048,1024]{1,0:T(8,128)}) %all-gather.13.cloned.1.call-update) | async-done | bytes 8388624 | tf_op jit(solution)/shard_map/all_gather | solution.py:50
  383.6 4.4 reduce_sum.185
  388.0 1.6 collective-permute-start.1
  389.6 6.5 %fusion.26 = f32[256,4096]{1,0:T(8,128)S(1)} fusion(bf16[1,1024,4096]{2,1,0:T(8,128)(2,1)} %param.12, bf16[3,256,1024]{2,1,0:T(8,128)(2,1)S(1)} %copy-done.18), kind=kOutput, calls=%fused_computation.36 | convolution fusion | flops 2148532224 | bytes 13107200 | tf_op jit(solution)/shard_map/dot_general | solution.py:44
  396.1 31.7 %all_gather.37 = bf16[256,1024]{1,0:T(8,128)(2,1)S(1)} all-gather(bf16[32,1024]{1,0:T(8,128)(2,1)S(1)} %bitcast_select_fusion), channel_id=1, replica_groups=mesh['section'=4,'tensor'=8] {'tensor'}, dimensions={0}, use_global_device_ids=true | all-gather | bytes 589824 | tf_op jit(solution)/shard_map/all_gather | solution.py:43
  427.9 2.4 fusion.38
  430.3 6.8 %fusion.6 = f32[256,1024]{1,0:T(8,128)} fusion(bf16[256,4096]{1,0:T(8,128)(2,1)S(1)} %fusion.38, bf16[1,1024,4096]{2,1,0:T(8,128)(2,1)} %param.12), kind=kOutput, calls=%fused_computation.20 | convolution fusion | flops 2147483648 | bytes 11534336 | tf_op jit(solution)/shard_map/tf,df->td/dot_general | solution.py:49
  437.0 0.0 all-gather.15.cloned.1.call-update
  437.1 7.1 %multiply_reduce_fusion.9 = f32[]{:T(128)} fusion(bf16[256,4096]{1,0:T(8,128)(2,1)} %copy-done.15, bf16[3,256,1024]{2,1,0:T(8,128)(2,1)} %all-gather.9.cloned.1.call-done, bf16[256]{0:T(256)(128)(2,1)S(1)} %get-tuple-element.11), kind=kOutput, calls=%fused_computation.11 | convolution fusion | flops 2156134400 | bytes 2621956 | tf_op jit(solution)/shard_map/td,tf->df/dot_general | solution.py:56
  444.3 5.6 multiply_reduce_fusion.8
  451.2 7.2 %multiply_reduce_fusion.11 = f32[]{:T(128)} fusion(bf16[256,4096]{1,0:T(8,128)(2,1)} %copy-done.15, bf16[3,256,1024]{2,1,0:T(8,128)(2,1)} %all-gather.9.cloned.1.call-done, bf16[256]{0:T(256)(128)(2,1)S(1)} %get-tuple-element.10), kind=kOutput, calls=%fused_computation.13 | convolution fusion | flops 2156134400 | bytes 2621956 | tf_op jit(solution)/shard_map/td,tf->df/dot_general | solution.py:56
  458.3 5.2 multiply_reduce_fusion.10
  464.8 0.1 pad_maximum_fusion.1
  464.9 7.3 %multiply_reduce_fusion.5 = f32[]{:T(128)} fusion(bf16[256,4096]{1,0:T(8,128)(2,1)} %copy-done.16, bf16[3,256,1024]{2,1,0:T(8,128)(2,1)} %all-gather.9.cloned.1.call-done, bf16[256]{0:T(256)(128)(2,1)S(1)} %get-tuple-element.9), kind=kOutput, calls=%fused_computation.7 | convolution fusion | flops 2156134400 | bytes 2621956 | tf_op jit(solution)/shard_map/td,tf->df/dot_general | solution.py:56
  472.2 5.2 multiply_reduce_fusion.4
  478.7 7.4 %multiply_reduce_fusion.7 = f32[]{:T(128)} fusion(bf16[256,4096]{1,0:T(8,128)(2,1)} %copy-done.16, bf16[3,256,1024]{2,1,0:T(8,128)(2,1)} %all-gather.9.cloned.1.call-done, bf16[256]{0:T(256)(128)(2,1)S(1)} %get-tuple-element.8), kind=kOutput, calls=%fused_computation.9 | convolution fusion | flops 2156134400 | bytes 2621956 | tf_op jit(solution)/shard_map/td,tf->df/dot_general | solution.py:56
  486.1 5.2 multiply_reduce_fusion.6
  492.5 0.1 pad_maximum_fusion.2
  492.6 6.4 %multiply_reduce_fusion.1 = f32[]{:T(128)} fusion(bf16[256,4096]{1,0:T(8,128)(2,1)S(1)} %fusion.38, bf16[3,256,1024]{2,1,0:T(8,128)(2,1)} %all-gather.9.cloned.1.call-done, bf16[256]{0:T(256)(128)(2,1)S(1)} %get-tuple-element.4), kind=kOutput, calls=%fused_computation.3 | convolution fusion | flops 2156134400 | bytes 2621956 | tf_op jit(solution)/shard_map/td,tf->df/dot_general | solution.py:56
  499.1 5.7 multiply_reduce_fusion
  506.0 6.4 %multiply_reduce_fusion.3 = f32[]{:T(128)} fusion(bf16[256,4096]{1,0:T(8,128)(2,1)S(1)} %fusion.38, bf16[3,256,1024]{2,1,0:T(8,128)(2,1)} %all-gather.9.cloned.1.call-done, bf16[256]{0:T(256)(128)(2,1)S(1)} %get-tuple-element.3), kind=kOutput, calls=%fused_computation.5 | convolution fusion | flops 2156134400 | bytes 2621956 | tf_op jit(solution)/shard_map/td,tf->df/dot_general | solution.py:56
  512.5 5.4 multiply_reduce_fusion.2
  519.1 0.1 pad_maximum_fusion.3
  519.1 19.2 %all-reduce = (f32[2]{0:T(128)S(1)}, f32[2]{0:T(128)S(1)}, f32[2]{0:T(128)S(1)}) all-reduce(f32[2]{0:T(128)S(1)} %pad_maximum_fusion.1, f32[2]{0:T(128)S(1)} %pad_maximum_fusion.2, f32[2]{0:T(128)S(1)} %pad_maximum_fusion.3), channel_id=1, replica_groups=mesh['section'=4,'tensor'=8] {'tensor'}, use_global_device_ids=true, to_apply=%region_5.6 | all-reduce | flops 6 | bytes 48 | tf_op jit(solution)/shard_map/psum | solution.py:64
  538.4 0.1 select_reduce_fusion.2
  538.5 0.1 select_reduce_fusion
  538.6 0.1 select_reduce_fusion.1
  538.6 10.1 %fusion.47 = f32[1024,4096]{1,0:T(8,128)} fusion(bf16[256,4096]{1,0:T(8,128)(2,1)} %copy-done.15, f32[256]{0:T(256)S(1)} %select_reduce_fusion.2, bf16[3,256,1024]{2,1,0:T(8,128)(2,1)} %all-gather.9.cloned.1.call-done), kind=kOutput, calls=%fused_computation.49 | convolution fusion | flops 2150629376 | bytes 19399680 | tf_op jit(solution)/shard_map/td,tf->df/dot_general | solution.py:69
  548.7 9.4 %fusion.48 = f32[1024,4096]{1,0:T(8,128)} fusion(bf16[256,4096]{1,0:T(8,128)(2,1)S(1)} %copy-done.17, f32[256]{0:T(256)S(1)} %select_reduce_fusion.1, bf16[3,256,1024]{2,1,0:T(8,128)(2,1)} %all-gather.9.cloned.1.call-done), kind=kOutput, calls=%fused_computation.50 | convolution fusion | flops 2150629376 | bytes 19399680 | tf_op jit(solution)/shard_map/td,tf->df/dot_general | solution.py:69
  558.1 8.2 %fusion.53 = f32[4096,1024]{1,0:T(8,128)} fusion(bf16[256,1024]{1,0:T(8,128)(2,1)S(1)} %copy-done.14, f32[256]{0:T(256)S(1)} %select_reduce_fusion.1, f32[256,4096]{1,0:T(8,128)S(1)} %copy-done.7), kind=kOutput, calls=%fused_computation.58 | convolution fusion | flops 2150367232 | bytes 21496832 | tf_op jit(solution)/shard_map/tf,td->fd/dot_general | solution.py:72
  566.3 8.2 %fusion.52 = f32[4096,1024]{1,0:T(8,128)} fusion(bf16[1,256,1024]{2,1,0:T(8,128)(2,1)S(1)} %all-gather, f32[256]{0:T(256)S(1)} %select_reduce_fusion.2, f32[256,4096]{1,0:T(8,128)S(1)} %copy-done.3), kind=kOutput, calls=%fused_computation.57 | convolution fusion | flops 2150367232 | bytes 21496832 | tf_op jit(solution)/shard_map/tf,td->fd/dot_general | solution.py:72
  574.5 15.6 %fusion.18 = bf16[1,1024,4096]{2,1,0:T(8,128)(2,1)} fusion(f32[1024,4096]{1,0:T(8,128)} %fusion.47, f32[1024,4096]{1,0:T(8,128)} %fusion.48, bf16[256,4096]{1,0:T(8,128)(2,1)S(1)} %fusion.38, f32[256]{0:T(256)S(1)} %select_reduce_fusion, bf16[3,256,1024]{2,1,0:T(8,128)(2,1)} %all-gather.9.cloned.1.call-done), kind=kOutput, calls=%fused_computation.32 | convolution fusion | flops 2163212288 | bytes 44565504 | tf_op jit(solution)/shard_map/td,tf->df/dot_general | solution.py:69
  590.1 16.8 %fusion.19 = bf16[1,4096,1024]{2,1,0:T(8,128)(2,1)} fusion(f32[4096,1024]{1,0:T(8,128)} %fusion.52, f32[4096,1024]{1,0:T(8,128)} %fusion.53, bf16[256,1024]{1,0:T(8,128)(2,1)S(1)} %all_gather.37, f32[256]{0:T(256)S(1)} %select_reduce_fusion, f32[256,4096]{1,0:T(8,128)} %copy-done.8), kind=kOutput, calls=%fused_computation.33 | convolution fusion | flops 2162950144 | bytes 46662656 | tf_op jit(solution)/shard_map/tf,td->fd/dot_general | solution.py:72
  606.9 4.4 reduce_sum.191
  611.4 0.7 maximum_bitcast_fusion
  (75 shorter events, 0.4 us)
Async XLA Ops:
  7.2 56.7 %all-gather.9.cloned.1.call-start = ((), (), s32[]{:S(2)}) async-start(), calls=%async_computation | async-start | bytes 1769472 | tf_op jit(solution)/shard_map/all_gather | solution.py:36
  16.0 189.7 %all-gather.11.cloned.1.call-start = ((), (), s32[]{:S(2)}) async-start(), calls=%async_computation.1 | async-start | bytes 9437184 | tf_op jit(solution)/shard_map/all_gather | solution.py:50
  63.9 14.8 %slice-start.4 = ((s8[8388608]{0:T(1024)(128)(4,1)}), s8[4194304]{0:T(1024)(128)(4,1)S(1)}, s32[]{:S(2)}) async-start(s8[8388608]{0:T(1024)(128)(4,1)} %bitcast.146), calls=%async_computation.8 | async-start | bytes 8388608
  69.9 7.4 %copy-start = (f32[256,4096]{1,0:T(8,128)}, f32[256,4096]{1,0:T(8,128)S(1)}, u32[]{:S(2)}) copy-start(f32[256,4096]{1,0:T(8,128)S(1)} %fusion.20) | copy-start | bytes 12582916
  70.0 8.8 %slice-start.5 = ((s8[8388608]{0:T(1024)(128)(4,1)}), s8[4194304]{0:T(1024)(128)(4,1)S(1)}, s32[]{:S(2)}) async-start(s8[8388608]{0:T(1024)(128)(4,1)} %bitcast.146), calls=%async_computation.9 | async-start | bytes 8388608
  77.4 1.4 copy-start.15
  82.1 301.5 %all-gather.13.cloned.1.call-start = ((), (), s32[]{:S(2)}) async-start(), calls=%async_computation.2 | async-start | bytes 9437184 | tf_op jit(solution)/shard_map/all_gather | solution.py:50
  205.8 4.5 copy-start.19
  205.8 6.1 copy-start.18
  210.3 39.9 %slice-start = ((s8[8388608]{0:T(1024)(128)(4,1)}), s8[4194304]{0:T(1024)(128)(4,1)S(1)}, s32[]{:S(2)}) async-start(s8[8388608]{0:T(1024)(128)(4,1)} %bitcast.142), calls=%async_computation.4 | async-start | bytes 8388608
  210.3 8.1 %copy-start.20 = (bf16[2,32,1024]{2,1,0:T(8,128)(2,1)S(1)}, bf16[2,32,1024]{2,1,0:T(8,128)(2,1)}, u32[]{:S(2)}) copy-start(bf16[2,32,1024]{2,1,0:T(8,128)(2,1)} %param.11) | copy-start | bytes 393220
  210.3 39.8 %slice-start.1 = ((s8[8388608]{0:T(1024)(128)(4,1)}), s8[4194304]{0:T(1024)(128)(4,1)S(1)}, s32[]{:S(2)}) async-start(s8[8388608]{0:T(1024)(128)(4,1)} %bitcast.142), calls=%async_computation.5 | async-start | bytes 8388608
  210.4 8.1 %collective-permute-start = (bf16[32,1024]{1,0:T(8,128)(2,1)S(1)}, bf16[32,1024]{1,0:T(8,128)(2,1)S(1)}, u32[]{:S(2)}, u32[]{:S(2)}) collective-permute-start(bf16[32,1024]{1,0:T(8,128)(2,1)S(1)} %fusion.81), channel_id=1, source_target_pairs={{8,0},{16,8},{24,16},{9,1},{17,9},{25,17},{10,2},{18,10},{26,18},{... | collective-permute-start | bytes 196616 | tf_op jit(solution)/shard_map/ppermute | solution.py:14
  218.4 34.1 %copy-start.4 = (f32[256,4096]{1,0:T(8,128)}, f32[256,4096]{1,0:T(8,128)S(1)}, u32[]{:S(2)}) copy-start(f32[256,4096]{1,0:T(8,128)S(1)} %fusion.23) | copy-start | bytes 12582916
  250.2 2.4 copy-start.11
  252.6 1.3 copy-start.16
  253.9 6.9 %copy-start.21 = (s32[1,3,2]{1,2,0:T(2,128)S(1)}, s32[1,3,2]{1,2,0:T(2,128)}, u32[]{:S(2)}) copy-start(s32[1,3,2]{1,2,0:T(2,128)} %param.9) | copy-start | bytes 76
  260.7 346.2 %all-gather.15.cloned.1.call-start = ((), (), s32[]{:S(2)}) async-start(), calls=%async_computation.3 | async-start | bytes 9437184 | tf_op jit(solution)/shard_map/all_gather | solution.py:50
  388.0 39.9 %slice-start.2 = ((s8[8388608]{0:T(1024)(128)(4,1)}), s8[4194304]{0:T(1024)(128)(4,1)S(1)}, s32[]{:S(2)}) async-start(s8[8388608]{0:T(1024)(128)(4,1)} %bitcast.144), calls=%async_computation.6 | async-start | bytes 8388608
  388.0 39.8 %slice-start.3 = ((s8[8388608]{0:T(1024)(128)(4,1)}), s8[4194304]{0:T(1024)(128)(4,1)S(1)}, s32[]{:S(2)}) async-start(s8[8388608]{0:T(1024)(128)(4,1)} %bitcast.144), calls=%async_computation.7 | async-start | bytes 8388608
  388.0 8.0 %collective-permute-start.1 = (bf16[32,1024]{1,0:T(8,128)(2,1)S(1)}, bf16[32,1024]{1,0:T(8,128)(2,1)S(1)}, u32[]{:S(2)}, u32[]{:S(2)}) collective-permute-start(bf16[32,1024]{1,0:T(8,128)(2,1)S(1)} %add_convert_fusion.3), channel_id=1, source_target_pairs={{8,0},{16,8},{24,16},{9,1},{17,9},{25,17},{10,2},{18,10},{26,18},{... | collective-permute-start | bytes 196616 | tf_op jit(solution)/shard_map/ppermute | solution.py:14
  396.1 34.2 %copy-start.8 = (f32[256,4096]{1,0:T(8,128)}, f32[256,4096]{1,0:T(8,128)S(1)}, u32[]{:S(2)}) copy-start(f32[256,4096]{1,0:T(8,128)S(1)} %fusion.26) | copy-start | bytes 12582916
  437.1 7.2 %copy-start.1 = (f32[256,4096]{1,0:T(8,128)S(1)}, f32[256,4096]{1,0:T(8,128)}, u32[]{:S(2)}) copy-start(f32[256,4096]{1,0:T(8,128)} %copy-done) | copy-start | bytes 12582916
  451.2 7.2 %copy-start.2 = (f32[256,4096]{1,0:T(8,128)S(1)}, f32[256,4096]{1,0:T(8,128)}, u32[]{:S(2)}) copy-start(f32[256,4096]{1,0:T(8,128)} %copy-done) | copy-start | bytes 12582916
  464.9 7.3 %copy-start.5 = (f32[256,4096]{1,0:T(8,128)S(1)}, f32[256,4096]{1,0:T(8,128)}, u32[]{:S(2)}) copy-start(f32[256,4096]{1,0:T(8,128)} %copy-done.4) | copy-start | bytes 12582916
  464.9 7.3 %copy-start.12 = (bf16[256,1024]{1,0:T(8,128)(2,1)S(1)}, bf16[256,1024]{1,0:T(8,128)(2,1)}, u32[]{:S(2)}) copy-start(bf16[256,1024]{1,0:T(8,128)(2,1)} %copy-done.11) | copy-start | bytes 1572868
  478.7 7.4 %copy-start.6 = (f32[256,4096]{1,0:T(8,128)S(1)}, f32[256,4096]{1,0:T(8,128)}, u32[]{:S(2)}) copy-start(f32[256,4096]{1,0:T(8,128)} %copy-done.4) | copy-start | bytes 12582916
  478.7 7.4 %copy-start.13 = (bf16[256,1024]{1,0:T(8,128)(2,1)S(1)}, bf16[256,1024]{1,0:T(8,128)(2,1)}, u32[]{:S(2)}) copy-start(bf16[256,1024]{1,0:T(8,128)(2,1)} %copy-done.11) | copy-start | bytes 1572868
  492.6 6.4 %copy-start.9 = (f32[256,4096]{1,0:T(8,128)S(1)}, f32[256,4096]{1,0:T(8,128)}, u32[]{:S(2)}) copy-start(f32[256,4096]{1,0:T(8,128)} %copy-done.8) | copy-start | bytes 12582916
  506.0 6.5 %copy-start.10 = (f32[256,4096]{1,0:T(8,128)S(1)}, f32[256,4096]{1,0:T(8,128)}, u32[]{:S(2)}) copy-start(f32[256,4096]{1,0:T(8,128)} %copy-done.8) | copy-start | bytes 12582916
  538.6 10.1 %copy-start.17 = (bf16[256,4096]{1,0:T(8,128)(2,1)S(1)}, bf16[256,4096]{1,0:T(8,128)(2,1)}, u32[]{:S(2)}) copy-start(bf16[256,4096]{1,0:T(8,128)(2,1)} %copy-done.16) | copy-start | bytes 6291460
  548.7 9.4 %copy-start.7 = (f32[256,4096]{1,0:T(8,128)S(1)}, f32[256,4096]{1,0:T(8,128)}, u32[]{:S(2)}) copy-start(f32[256,4096]{1,0:T(8,128)} %copy-done.4) | copy-start | bytes 12582916
  548.7 9.4 %copy-start.14 = (bf16[256,1024]{1,0:T(8,128)(2,1)S(1)}, bf16[256,1024]{1,0:T(8,128)(2,1)}, u32[]{:S(2)}) copy-start(bf16[256,1024]{1,0:T(8,128)(2,1)} %copy-done.11) | copy-start | bytes 1572868
  558.1 8.2 %copy-start.3 = (f32[256,4096]{1,0:T(8,128)S(1)}, f32[256,4096]{1,0:T(8,128)}, u32[]{:S(2)}) copy-start(f32[256,4096]{1,0:T(8,128)} %copy-done) | copy-start | bytes 12582916
Sparse Core Ops, SparseCore 0:
  16.2 47.6 all-gather.8
  82.2 123.5 all-gather.10
  260.8 122.7 all-gather.12
  437.2 123.1 all-gather.14
